TPU v7x, 32 devices: a whole 2x2x4 slice. The times are simulated.
32 devices in a mesh: kpt: 4 (over z), row: 2 (over x), col: 4 (over y, core).
Axes of the slice: x: 2, y: 2, z: 4, core: 2. Of those that a mesh axis runs over, the one named last changes fastest.
Arguments:
- occ_orbitals: bfloat16 [4, 2048, 256], P('kpt', 'row'), may hold values from -6 to 6
- empty_orbitals: bfloat16 [4, 2048, 896], P('kpt', 'row'), may hold values from -6 to 6
- occ_energy: float32 [4, 256], replicated, may hold values from 0.05 to 2
- empty_energy: float32 [4, 896], replicated, may hold values from 0.05 to 2
- tau_points: float32 [3], replicated, may hold values from 0.3 to 3
- partner: int32 [4], replicated, may hold values from 0 to 3, each once
- mirror: int32 [2048], P('col'), may hold values from 0 to 2047, each once
Outputs:
- polarization: float32 [3, 2, 1024, 2048], P(None, 'row', 'kpt', 'col')
Inputs may be any that keep to these rules, and one draw needn't show every extreme that they name: Each k-point is the partner of exactly one k-point. `mirror`: each grid point is the column of exactly one window column.
All inputs are finite; a program needn't handle non-finite values.
Results may differ from a plain program's by a relative error of at most 0.0003.
Values may be sent and summed in bfloat16 or wider, within the bound.
A program may use at most 64 MiB of HBM per device.

v0:
```python
import functools
import math

import jax
import jax.numpy as jnp
from jax import lax
from jax.experimental import pallas as pl
from jax.experimental.pallas import tpu as pltpu
from jax.sharding import PartitionSpec as P

NOCC = 256
NEMP = 896
TAUS = 3
EXCHANGE_BYTES = 24 * 2**20


def green_tile(rows, cols, weight, width):
    scaled = (rows.astype(jnp.float32) * weight[None, :]).astype(jnp.bfloat16)
    tile = lax.dot_general(
        scaled, cols, (((1,), (1,)), ((), ())), preferred_element_type=jnp.float32
    )
    return tile * (1.0 / math.sqrt(width))


def permute_block(block, source):
    spread = lax.all_to_all(block, "kpt", split_axis=1, concat_axis=0, tiled=True)
    arranged = jnp.take(spread, source, axis=0)
    return lax.all_to_all(arranged, "kpt", split_axis=0, concat_axis=1, tiled=True)


def shards_reduced(occ_orbitals, empty_orbitals, occ_energy, empty_energy, tau_points, partner, mirror):
    kpoints = lax.axis_size("kpt")
    own_index = lax.axis_index("kpt")
    kpoint_ids = jnp.arange(kpoints, dtype=jnp.int32)
    matches = partner[None, :] == kpoint_ids[:, None]
    inverse = jnp.sum(jnp.where(matches, kpoint_ids[None, :], 0), axis=1)
    occ_block = permute_block(occ_orbitals, inverse)
    occ_kpoint = inverse[own_index]
    occ_rows = occ_block[0]
    empty_rows = empty_orbitals[0]
    occ_levels = lax.dynamic_index_in_dim(occ_energy, occ_kpoint, 0, keepdims=False)
    empty_levels = lax.dynamic_index_in_dim(empty_energy, own_index, 0, keepdims=False)
    occ_full, empty_full = (
        lax.all_gather(occ_rows, "row", axis=0, tiled=True),
        lax.all_gather(empty_rows, "row", axis=0, tiled=True),
    )
    occ_cols = jnp.take(occ_full, mirror, axis=0)
    empty_cols = jnp.take(empty_full, mirror, axis=0)
    factor = -1.0 / math.sqrt(kpoints)
    slabs = []
    for time_index in range(TAUS):
        occ_weight = jnp.exp(-tau_points[time_index] * occ_levels)
        empty_weight = jnp.exp(-tau_points[time_index] * empty_levels)
        occ_green = green_tile(occ_rows, occ_cols, occ_weight, NOCC)
        empty_green = green_tile(empty_rows, empty_cols, empty_weight, NEMP)
        slabs.append(occ_green * empty_green * factor)
    product_term = jnp.stack(slabs, axis=0)[:, None, :, :]
    return lax.psum_scatter(product_term, "kpt", scatter_dimension=2, tiled=True)


def exchange_kernel(kpoints, columns, half_ref, rows_ref, cols_out, rows_out,
                    local_sem, send_c, recv_c, send_r, recv_r, send_x, recv_x, send_f, recv_f):
    me, own_row, own_col = lax.axis_index("kpt"), lax.axis_index("row"), lax.axis_index("col")
    part = rows_out.shape[2]
    slab = part * columns

    def remote(src, dst, send_sem, recv_sem, device):
        copy = pltpu.make_async_remote_copy(
            src_ref=src, dst_ref=dst, send_sem=send_sem, recv_sem=recv_sem,
            device_id=device, device_id_type=pl.DeviceIdType.MESH,
        )
        copy.start()
        return copy

    barrier = pltpu.get_barrier_semaphore()
    peers = [{"kpt": lax.rem(me + d, kpoints)} for d in range(1, kpoints)]
    peers += [{"row": 1 - own_row}]
    peers += [{"col": lax.rem(own_col + e, columns)} for e in range(1, columns)]
    for peer in peers:
        pl.semaphore_signal(barrier, inc=1, device_id=peer, device_id_type=pl.DeviceIdType.MESH)
    pl.semaphore_wait(barrier, len(peers))

    across = {"row": 1 - own_row}
    col_copies, row_copies, pending = [], [], []
    for d in range(1, kpoints):
        other = lax.rem(me + d, kpoints)
        col_copies.append(remote(half_ref, cols_out.at[me, own_row], send_c.at[d], recv_c.at[d], {"kpt": other}))
    pending.append(remote(half_ref, cols_out.at[me, own_row], send_x.at[0], recv_x.at[0], across))
    for d in range(1, kpoints):
        other = lax.rem(me + d, kpoints)
        start = pl.multiple_of((other * columns + own_col) * part, part)
        row_copies.append(remote(rows_ref.at[pl.ds(start, part), :], rows_out.at[me, own_col], send_r.at[d], recv_r.at[d], {"kpt": other}))
    local = [pltpu.make_async_copy(half_ref, cols_out.at[me, own_row], local_sem.at[0])]
    for c in range(columns):
        start = pl.multiple_of(me * slab + c * part, part)
        local.append(pltpu.make_async_copy(rows_ref.at[pl.ds(start, part), :], rows_out.at[me, c], local_sem.at[1 + c]))
    for copy in local:
        copy.start()

    order = sorted(range(1, kpoints), key=lambda d: min(d, kpoints - d))
    for d in order:
        source = lax.rem(me + kpoints - d, kpoints)
        col_copies[d - 1].wait_recv()
        held = cols_out.at[source, own_row]
        pending.append(remote(held, held, send_x.at[d], recv_x.at[d], across))
    for d in order:
        source = lax.rem(me + kpoints - d, kpoints)
        row_copies[d - 1].wait_recv()
        held = rows_out.at[source, own_col]
        for e in range(1, columns):
            pending.append(remote(held, held, send_f.at[d, e], recv_f.at[d, e], {"col": lax.rem(own_col + e, columns)}))
    for copy in local:
        copy.wait()
    for copy in col_copies + row_copies:
        copy.wait_send()
    for copy in pending:
        copy.wait()


def exchange(half, rows, kpoints, columns):
    points, width = half.shape
    part = rows.shape[0] // (kpoints * columns)
    dma = pltpu.SemaphoreType.DMA
    vmem = pl.BlockSpec(memory_space=pltpu.VMEM)
    return pl.pallas_call(
        functools.partial(exchange_kernel, kpoints, columns),
        out_shape=(
            jax.ShapeDtypeStruct((kpoints, 2, points, width), half.dtype),
            jax.ShapeDtypeStruct((kpoints, columns, part, width), rows.dtype),
        ),
        in_specs=[vmem, vmem],
        out_specs=(vmem, vmem),
        scratch_shapes=[
            dma((1 + columns,)),
            dma((kpoints,)), dma((kpoints,)),
            dma((kpoints,)), dma((kpoints,)),
            dma((kpoints,)), dma((kpoints,)),
            dma((kpoints, columns)), dma((kpoints, columns)),
        ],
        compiler_params=pltpu.CompilerParams(collective_id=0, has_side_effects=True),
        name="exchange",
    )(half, rows)


def green_batch(rows, cols, weights):
    kpoints, slab, width = rows.shape
    scaled = (rows.astype(jnp.float32)[:, None] * weights[:, :, None, :]).astype(jnp.bfloat16)
    scaled = scaled.reshape(kpoints, -1, width)
    return lax.dot_general(scaled, cols, (((2,), (2,)), ((0,), (0,))), preferred_element_type=jnp.float32)


def products(partner, rows, cols, weights, nocc, scale):
    kpoints, slab, width = rows.shape
    occ = green_batch(rows[:, :, :nocc], cols[:, :, :nocc], weights[:, :, :nocc])
    empty = green_batch(
        jnp.take(rows[:, :, nocc:], partner, axis=0, mode="clip"),
        jnp.take(cols[:, :, nocc:], partner, axis=0, mode="clip"),
        jnp.take(weights[:, :, nocc:], partner, axis=0, mode="clip"),
    )
    total = jnp.sum(occ * empty, axis=0) * scale
    return total.reshape(-1, slab, cols.shape[1])


def shards_exchanged(occ_orbitals, empty_orbitals, occ_energy, empty_energy, tau_points, partner, mirror):
    kpoints, columns = lax.axis_size("kpt"), lax.axis_size("col")
    own_row = lax.axis_index("row")
    rows = jnp.concatenate([occ_orbitals[0], empty_orbitals[0]], axis=1)
    nrows, width = rows.shape
    window = mirror.shape[0]
    points = window // 2
    index = mirror - own_row * nrows
    mine = lax.dynamic_slice_in_dim(index, own_row * points, points)
    theirs = lax.dynamic_slice_in_dim(index, (1 - own_row) * points, points)
    clipped = jnp.clip(jnp.concatenate([theirs, mine]), 0, nrows - 1)
    picked = rows.at[clipped].get(mode="promise_in_bounds")
    arrived = lax.ppermute(picked[:points], "row", [(0, 1), (1, 0)])
    here = (mine >= 0) & (mine < nrows)
    half = jnp.where(here[:, None], picked[points:], arrived)
    cols, slabs = exchange(half, rows, kpoints, columns)
    energy = jnp.concatenate([occ_energy, empty_energy], axis=1)
    weights = jnp.exp(-tau_points[None, :, None] * energy[:, None, :])
    scale = -1.0 / math.sqrt(kpoints) / math.sqrt(NOCC) / math.sqrt(NEMP)
    total = products(
        partner,
        slabs.reshape(kpoints, nrows // kpoints, width),
        cols.reshape(kpoints, window, width),
        weights,
        occ_orbitals.shape[2],
        scale,
    )
    return total[:, None]


def shards(*args):
    kpoints, columns = lax.axis_size("kpt"), lax.axis_size("col")
    nrows, width = args[0].shape[1], args[0].shape[2] + args[1].shape[2]
    window = args[6].shape[0]
    held = 2 * width * (kpoints * window + 2 * nrows)
    part = nrows // (kpoints * columns)
    fits = held <= EXCHANGE_BYTES and part % 16 == 0 and window % 32 == 0
    if lax.axis_size("row") == 2 and fits:
        return shards_exchanged(*args)
    return shards_reduced(*args)


def solution(mesh):
    return jax.shard_map(
        shards,
        mesh=mesh,
        in_specs=(P("kpt", "row", None), P("kpt", "row", None), P(), P(), P(), P(), P("col")),
        out_specs=P(None, "row", "kpt", "col"),
        check_vma=False,
    )
```

profile of v0, /device:TPU:8, one launch (start us, length us, event | category | flops | bytes accessed | tf_op | source)
XLA Modules:
  0.0 149.3 jit_solution(13133209991052251016)
XLA Ops:
  0.0 0.7 broadcast_subtract_fusion
  0.7 0.7 compare_and_fusion
  1.3 0.1 dynamic_slice.7
  1.4 0.6 pad_clamp_fusion.1
  2.0 1.8 %pad_maximum_fusion.rows_ref = bf16[1024,1152]{1,0:T(8,128)(2,1)S(1)} fusion(bf16[1024,896]{1,0:T(8,128)(2,1)} %bitcast.21, bf16[1024,256]{1,0:T(8,128)(2,1)} %bitcast.22), kind=kLoop, calls=%fused_computation.7 | loop fusion | flops 4718592 | bytes 4718592 | tf_op jit(solution)/shard_map/concatenate | solution.py:167
  3.8 0.0 copy-start
  3.8 0.0 copy-start.4
  3.8 2.4 %gather_fusion = bf16[512,1152]{1,0:T(8,128)(2,1)S(1)} fusion(bf16[1024,1152]{1,0:T(8,128)(2,1)S(1)} %pad_maximum_fusion.rows_ref, s32[1024]{0:T(1024)} %pad_clamp_fusion.1), kind=kCustom, calls=%fused_computation | custom fusion | bytes 2361344 | tf_op jit(solution)/shard_map/gather | solution.py:175
  6.2 0.0 copy-done
  6.2 0.9 slice.41
  7.1 1.5 collective-permute-start
  8.6 0.0 copy-done.4
  8.6 0.7 pad_maximum_fusion.1
  9.3 0.7 neg.4
  9.9 0.1 multiply_exponential_fusion
  10.0 0.0 copy-start.3
  10.1 0.7 pad_clamp_fusion
  10.7 0.6 gather_fusion.2
  11.3 11.0 %collective-permute-done = bf16[256,1152]{1,0:T(8,128)(2,1)S(1)} collective-permute-done((bf16[256,1152]{1,0:T(8,128)(2,1)}, bf16[256,1152]{1,0:T(8,128)(2,1)S(1)}, u32[]{:S(2)}, u32[]{:S(2)}) %collective-permute-start) | collective-permute-done | bytes 589856 | tf_op jit(solution)/shard_map/ppermute | solution.py:176
  22.4 1.6 %slice_select_fusion.half_ref = bf16[256,1152]{1,0:T(8,128)(2,1)} fusion(bf16[256,1152]{1,0:T(8,128)(2,1)S(1)} %collective-permute-done, bf16[512,1152]{1,0:T(8,128)(2,1)S(1)} %gather_fusion, pred[256]{0:T(512)(128)(4,1)} %get-tuple-element.9), kind=kLoop, calls=%fused_computation.11 | loop fusion | flops 294912 | bytes 1769728 | tf_op jit(solution)/shard_map/jit(_where)/select_n | solution.py:178
  24.0 93.5 %exchange.1 = (bf16[4,2,256,1152]{3,2,1,0:T(8,128)(2,1)}, bf16[4,4,64,1152]{3,2,1,0:T(8,128)(2,1)}) custom-call(bf16[256,1152]{1,0:T(8,128)(2,1)} %slice_select_fusion.half_ref, bf16[1024,1152]{1,0:T(8,128)(2,1)} %copy-done), custom_call_target="tpu_custom_call" | custom-call | tf_op jit(solution)/shard_map/exchange/pallas_call | solution.py:125
  117.5 1.6 %slice.45 = bf16[4,256,896]{2,1,0:T(8,128)(2,1)S(1)} slice(bf16[4,256,1152]{2,1,0:T(8,128)(2,1)} %bitcast.19), slice={[0:4], [0:256], [256:1152]} | slice | bytes 3670016 | tf_op jit(solution)/shard_map/slice | solution.py:156
  119.1 0.0 copy-done.3
  119.1 1.1 slice_convert_fusion
  120.3 2.0 %gather_fusion.1 = bf16[4,256,896]{2,1,0:T(8,128)(2,1)} fusion(bf16[4,256,896]{2,1,0:T(8,128)(2,1)S(1)} %slice.45, s32[1024]{0:T(1024)S(1)} %pad_clamp_fusion), kind=kCustom, calls=%fused_computation.1 | custom fusion | bytes 3670032 | tf_op jit(solution)/shard_map/jit(_take)/gather | solution.py:156
  122.2 0.0 copy-start.1
  122.2 3.7 %convert_element_type.27 = f32[4,256,896]{2,1,0:T(8,128)} convert(bf16[4,256,896]{2,1,0:T(8,128)(2,1)} %gather_fusion.1) | non-fusion elementwise | flops 917504 | bytes 5505024 | tf_op jit(solution)/shard_map/convert_element_type | solution.py:147
  126.0 0.0 copy-done.1
  126.0 0.0 slice-start.2
  126.0 2.2 %slice.47 = bf16[4,512,896]{2,1,0:T(8,128)(2,1)} slice(bf16[4,512,1152]{2,1,0:T(8,128)(2,1)S(1)} %bitcast.17), slice={[0:4], [0:512], [256:1152]} | slice | bytes 7340032 | tf_op jit(solution)/shard_map/slice | solution.py:157
  128.2 0.0 slice-done.2
  128.2 0.3 multiply_convert_fusion.1
  128.5 3.7 %fusion = f32[4,768,512]{2,1,0:T(8,128)} fusion(bf16[4,768,256]{2,1,0:T(8,128)(2,1)S(1)} %bitcast.15, bf16[4,512,1152]{2,1,0:T(8,128)(2,1)S(1)} %bitcast.18), kind=kOutput, calls=%fused_computation.8 | convolution fusion | flops 805306368 | bytes 8912896 | tf_op jit(solution)/shard_map/dot_general | solution.py:149
  132.2 0.0 slice-start
  132.2 4.9 %gather_fusion.3 = bf16[4,512,896]{2,1,0:T(8,128)(2,1)} fusion(bf16[4,512,896]{2,1,0:T(8,128)(2,1)} %slice.47, s32[1024]{0:T(1024)S(1)} %pad_clamp_fusion), kind=kCustom, calls=%fused_computation.3 | custom fusion | bytes 7340048 | tf_op jit(solution)/shard_map/jit(_take)/gather | solution.py:157
  137.1 0.0 slice-start.1
  137.1 0.0 copy-start.2
  137.1 3.4 %multiply_convert_fusion = bf16[4,3,256,896]{3,2,1,0:T(8,128)(2,1)S(1)} fusion(f32[4,3,896]{2,1,0:T(4,128)S(1)} %gather_fusion.2, f32[4,256,896]{2,1,0:T(8,128)} %convert_element_type.27), kind=kLoop, calls=%fused_computation.4 | loop fusion | flops 5505024 | bytes 9218048 | tf_op jit(solution)/shard_map/convert_element_type | solution.py:147
  140.5 0.0 slice-done
  140.5 0.0 slice-done.1
  140.5 1.0 copy-done.2
  141.5 5.0 %multiply_reduce_fusion = f32[768,512]{1,0:T(8,128)} fusion(f32[4,768,512]{2,1,0:T(8,128)S(1)} %bitcast.14, bf16[4,768,896]{2,1,0:T(8,128)(2,1)S(1)} %bitcast.16, bf16[4,512,896]{2,1,0:T(8,128)(2,1)S(1)} %copy-done.2), kind=kOutput, calls=%fused_computation.5 | convolution fusion | flops 2821324800 | bytes 17039360 | tf_op jit(solution)/shard_map/dot_general | solution.py:149
  146.5 2.7 %broadcast_multiply_fusion = f32[768,512]{1,0:T(8,128)} fusion(f32[768,512]{1,0:T(8,128)} %multiply_reduce_fusion), kind=kLoop, calls=%fused_computation.10 | loop fusion | flops 393216 | bytes 3145728 | tf_op jit(solution)/shard_map/mul | solution.py:160
  (3 shorter events, 0.0 us)
Async XLA Ops:
  3.8 2.4 %copy-start = (bf16[1024,1152]{1,0:T(8,128)(2,1)}, bf16[1024,1152]{1,0:T(8,128)(2,1)S(1)}, u32[]{:S(2)}) copy-start(bf16[1024,1152]{1,0:T(8,128)(2,1)S(1)} %pad_maximum_fusion.rows_ref) | copy-start | bytes 7077892
  3.8 4.8 %copy-start.4 = (f32[4,896]{1,0:T(4,128)S(1)}, f32[4,896]{1,0:T(4,128)}, u32[]{:S(2)}) copy-start(f32[4,896]{1,0:T(4,128)} %param.10) | copy-start | bytes 43012
  7.1 15.3 %collective-permute-start = (bf16[256,1152]{1,0:T(8,128)(2,1)}, bf16[256,1152]{1,0:T(8,128)(2,1)S(1)}, u32[]{:S(2)}, u32[]{:S(2)}) collective-permute-start(bf16[256,1152]{1,0:T(8,128)(2,1)} %slice.41), channel_id=1, source_target_pairs={{0,4},{4,0},{1,5},{5,1},{2,6},{6,2},{3,7},{7,3},{8,12},{12,8},{9,1... | collective-permute-start | bytes 1769480 | tf_op jit(solution)/shard_map/ppermute | solution.py:176
  10.0 109.1 %copy-start.3 = (f32[4,3,1152]{2,1,0:T(4,128)}, f32[4,3,1152]{2,1,0:T(4,128)S(1)}, u32[]{:S(2)}) copy-start(f32[4,3,1152]{2,1,0:T(4,128)S(1)} %multiply_exponential_fusion) | copy-start | bytes 165892
  122.2 3.7 %copy-start.1 = (bf16[4,2,256,1152]{3,2,1,0:T(8,128)(2,1)S(1)}, bf16[4,2,256,1152]{3,2,1,0:T(8,128)(2,1)}, u32[]{:S(2)}) copy-start(bf16[4,2,256,1152]{3,2,1,0:T(8,128)(2,1)} %get-tuple-element.8) | copy-start | bytes 14155780
  126.0 2.2 %slice-start.2 = ((f32[4,3,1152]{2,1,0:T(4,128)}), f32[4,3,256]{2,1,0:T(4,128)S(1)}, s32[]{:S(2)}) async-start(f32[4,3,1152]{2,1,0:T(4,128)} %copy-done.3), calls=%async_computation.2 | async-start | bytes 32768 | tf_op jit(solution)/shard_map/slice | solution.py:154
  132.2 8.3 %slice-start = ((s8[6291456]{0:T(1024)(128)(4,1)}), s8[2097152]{0:T(1024)(128)(4,1)S(1)}, s32[]{:S(2)}) async-start(s8[6291456]{0:T(1024)(128)(4,1)} %bitcast.13), calls=%async_computation | async-start | bytes 4194304
  137.1 3.4 %slice-start.1 = ((s8[6291456]{0:T(1024)(128)(4,1)}), s8[4194304]{0:T(1024)(128)(4,1)S(1)}, s32[]{:S(2)}) async-start(s8[6291456]{0:T(1024)(128)(4,1)} %bitcast.13), calls=%async_computation.1 | async-start | bytes 8388608
  137.1 4.4 %copy-start.2 = (bf16[4,512,896]{2,1,0:T(8,128)(2,1)S(1)}, bf16[4,512,896]{2,1,0:T(8,128)(2,1)}, u32[]{:S(2)}) copy-start(bf16[4,512,896]{2,1,0:T(8,128)(2,1)} %gather_fusion.3) | copy-start | bytes 11010052
where the time goes:
time: 150 us; the launch traced here: 149 us
  Pallas kernels  93.5 us (62%)
  other arithmetic  18.7 us (12%)
  local copies, waits for them, and re-layouts  15.7 us (10%)
  waiting for transfers between devices  11 us (7%)
  matrix products  8.68 us (6%)
    pallas_call x1, Pallas kernels, exchange(): pl.pallas_call(functools.partial(exchange_kernel, kpoints, columns), out_...  93.5 us
    ppermute x1, waiting for transfers between devices, shards_exchanged(): arrived = lax.ppermute(picked[:points], 'row', [(0, 1), (1, 0)])  11 us
    dot_general x2, matrix products, green_batch(): lax.dot_general(scaled, cols, (((2,), (2,)), ((0,), (0,))), preferred_ele...  8.68 us
    gather x1, local copies, waits for them, and re-layouts, products(): jnp.take(cols[:, :, nocc:], partner, axis=0, mode='clip')  4.93 us
    convert_element_type x2, other arithmetic, green_batch(): rows.astype(jnp.float32)[:, None] * weights[:, :, None, :]  4.86 us
    convert_element_type x2, other arithmetic, green_batch(): (rows.astype(jnp.float32)[:, None] * weights[:, :, None, :]).astype(jnp.b...  3.69 us
  transfers between devices with their start and end apart: 1, of which 1 were waited for; matrix products, arithmetic and copies ran while one was open for 2% of the time, Pallas kernels for 0%

commit v1 on v0

v1 whole, which is shorter than its diff:
```python
import functools
import math

import jax
import jax.numpy as jnp
from jax import lax
from jax.experimental import pallas as pl
from jax.experimental.pallas import tpu as pltpu
from jax.sharding import PartitionSpec as P

NOCC = 256
NEMP = 896
TAUS = 3
LINE_BYTES = 40 * 2**20
CHUNKS = 4
LANES = 128
TILE = 16


def green_tile(rows, cols, weight, width):
    scaled = (rows.astype(jnp.float32) * weight[None, :]).astype(jnp.bfloat16)
    tile = lax.dot_general(
        scaled, cols, (((1,), (1,)), ((), ())), preferred_element_type=jnp.float32
    )
    return tile * (1.0 / math.sqrt(width))


def permute_block(block, source):
    spread = lax.all_to_all(block, "kpt", split_axis=1, concat_axis=0, tiled=True)
    arranged = jnp.take(spread, source, axis=0)
    return lax.all_to_all(arranged, "kpt", split_axis=0, concat_axis=1, tiled=True)


def shards_reduced(occ_orbitals, empty_orbitals, occ_energy, empty_energy, tau_points, partner, mirror):
    kpoints = lax.axis_size("kpt")
    own_index = lax.axis_index("kpt")
    kpoint_ids = jnp.arange(kpoints, dtype=jnp.int32)
    matches = partner[None, :] == kpoint_ids[:, None]
    inverse = jnp.sum(jnp.where(matches, kpoint_ids[None, :], 0), axis=1)
    occ_block = permute_block(occ_orbitals, inverse)
    occ_kpoint = inverse[own_index]
    occ_rows = occ_block[0]
    empty_rows = empty_orbitals[0]
    occ_levels = lax.dynamic_index_in_dim(occ_energy, occ_kpoint, 0, keepdims=False)
    empty_levels = lax.dynamic_index_in_dim(empty_energy, own_index, 0, keepdims=False)
    occ_full, empty_full = (
        lax.all_gather(occ_rows, "row", axis=0, tiled=True),
        lax.all_gather(empty_rows, "row", axis=0, tiled=True),
    )
    occ_cols = jnp.take(occ_full, mirror, axis=0)
    empty_cols = jnp.take(empty_full, mirror, axis=0)
    factor = -1.0 / math.sqrt(kpoints)
    slabs = []
    for time_index in range(TAUS):
        occ_weight = jnp.exp(-tau_points[time_index] * occ_levels)
        empty_weight = jnp.exp(-tau_points[time_index] * empty_levels)
        occ_green = green_tile(occ_rows, occ_cols, occ_weight, NOCC)
        empty_green = green_tile(empty_rows, empty_cols, empty_weight, NEMP)
        slabs.append(occ_green * empty_green * factor)
    product_term = jnp.stack(slabs, axis=0)[:, None, :, :]
    return lax.psum_scatter(product_term, "kpt", scatter_dimension=2, tiled=True)


def line_kernel(kpoints, columns, scale,
                tau_ref, partner_ref, mirror_ref, occ_energy_ref, empty_energy_ref, occ_ref, empty_ref, out_ref,
                cols, mine, pre_out, pre_in, rows_occ, rows_empty, scaled_occ, scaled_empty, green_occ, green_empty,
                send_p, recv_p, send_r, recv_r, send_f, recv_f,
                send_u, recv_u, send_d, recv_d, send_x, recv_x):
    me, own_row, own_col = lax.axis_index("kpt"), lax.axis_index("row"), lax.axis_index("col")
    nrows, nocc = occ_ref.shape
    width = nocc + empty_ref.shape[1]
    slab = nrows // kpoints
    part = slab // columns
    half = mine.shape[0]
    size = half // CHUNKS
    times = tau_ref.shape[0]
    last = kpoints - 1
    across = {"row": 1 - own_row}
    above, below = {"kpt": lax.rem(me + 1, kpoints)}, {"kpt": lax.rem(me + last, kpoints)}

    def remote(src, dst, send_sem, recv_sem, device):
        return pltpu.make_async_remote_copy(
            src_ref=src, dst_ref=dst, send_sem=send_sem, recv_sem=recv_sem,
            device_id=device, device_id_type=pl.DeviceIdType.MESH,
        )

    barrier = pltpu.get_barrier_semaphore()
    peers = [{"kpt": lax.rem(me + d, kpoints)} for d in range(1, kpoints)]
    peers += [across]
    peers += [{"col": lax.rem(own_col + e, columns)} for e in range(1, columns)]
    for peer in peers:
        pl.semaphore_signal(barrier, inc=1, device_id=peer, device_id_type=pl.DeviceIdType.MESH)
    pl.semaphore_wait(barrier, len(peers))

    def row_copies(d):
        other = lax.rem(me + d, kpoints)
        start = pl.multiple_of((other * columns + own_col) * part, part)
        return [
            remote(src.at[pl.ds(start, part), :], dst.at[me, own_col], send_r.at[i, d], recv_r.at[i, d], {"kpt": other})
            for i, (src, dst) in enumerate(((occ_ref, rows_occ), (empty_ref, rows_empty)))
        ]

    def row_forwards(d):
        source = lax.rem(me + kpoints - d, kpoints)
        return [
            remote(dst.at[source, own_col], dst.at[source, own_col], send_f.at[i, d, e], recv_f.at[i, d, e],
                   {"col": lax.rem(own_col + e, columns)})
            for e in range(1, columns)
            for i, dst in enumerate((rows_occ, rows_empty))
        ]

    def pre_copy(c):
        piece = pl.ds(c * size, size)
        return remote(pre_out.at[piece], pre_in.at[piece], send_p.at[c], recv_p.at[c], across)

    def cross_copy(k, c):
        piece = cols.at[k, own_row, pl.ds(c * size, size)]
        return remote(piece, piece, send_x.at[k, c], recv_x.at[k, c], across)

    def up_copy(s, c):
        piece = cols.at[lax.rem(me - s + kpoints, kpoints), own_row, pl.ds(c * size, size)]
        return remote(piece, piece, send_u.at[s, c], recv_u.at[s, c], above)

    def down_copy(s, c):
        piece = cols.at[lax.rem(me + s, kpoints), own_row, pl.ds(c * size, size)]
        return remote(piece, piece, send_d.at[s, c], recv_d.at[s, c], below)

    for d in range(1, kpoints):
        for copy in row_copies(d):
            copy.start()

    def pick(first):
        index = mirror_ref[0:1, pl.ds(pl.multiple_of(first, LANES), LANES)] - own_row * nrows
        index = jnp.transpose(jnp.broadcast_to(index, (LANES, LANES)))
        lane = lax.broadcasted_iota(jnp.int32, (LANES, LANES), 1)
        hot = jnp.concatenate(
            [jnp.where(index == lane + b, 1.0, 0.0).astype(jnp.bfloat16) for b in range(0, nrows, LANES)], axis=1)
        dot = functools.partial(jnp.dot, hot, preferred_element_type=jnp.float32)
        return dot(occ_ref[...]).astype(jnp.bfloat16), dot(empty_ref[...]).astype(jnp.bfloat16)

    def fill(dst, whose):
        for first in range(0, half, LANES):
            occ, empty = pick(whose * half + first)
            dst[first:first + LANES, :nocc] = occ
            dst[first:first + LANES, nocc:] = empty
            yield range(first // size, (first + LANES) // size)

    for chunks in fill(pre_out, 1 - own_row):
        for c in chunks:
            pre_copy(c).start()
    for _ in fill(mine, own_row):
        pass

    for c in range(columns):
        start = pl.multiple_of(me * slab + c * part, part)
        rows_occ[me, c] = occ_ref[pl.ds(start, part), :]
        rows_empty[me, c] = empty_ref[pl.ds(start, part), :]

    def scale_rows(k):
        for rows, energy, scaled in ((rows_occ, occ_energy_ref, scaled_occ), (rows_empty, empty_energy_ref, scaled_empty)):
            held = energy[...]
            pick_k = lax.broadcasted_iota(jnp.int32, held.shape, 0) == k
            levels = jnp.sum(jnp.where(pick_k, held, 0.0), axis=0, keepdims=True)
            weights = [jnp.exp(-tau_ref[t] * levels) for t in range(times)]

            @pl.loop(0, columns)
            def _(c):
                block = rows[k, c].astype(jnp.float32)
                for t in range(times):
                    start = pl.multiple_of(t * slab + c * part, part)
                    scaled[k, pl.ds(start, part), :] = (block * weights[t]).astype(jnp.bfloat16)

    def multiply(k, h):
        window = pl.ds(pl.multiple_of(h * half, half), half)

        @pl.loop(0, times)
        def _(t):
            rows = pl.ds(pl.multiple_of(t * slab, slab), slab)
            for scaled, green, lo, hi in ((scaled_occ, green_occ, 0, nocc), (scaled_empty, green_empty, nocc, width)):
                green[k, rows, window] = lax.dot_general(
                    scaled[k, rows, :], cols[k, h, :, lo:hi], (((1,), (1,)), ((), ())),
                    preferred_element_type=jnp.float32)

    def combine(h):
        window = pl.ds(pl.multiple_of(h * half, half), half)

        @pl.loop(0, times * slab, step=TILE)
        def _(start):
            rows = pl.ds(pl.multiple_of(start, TILE), TILE)
            total = green_occ[0, rows, window] * green_empty[partner_ref[0], rows, window]
            for k in range(1, kpoints):
                total += green_occ[k, rows, window] * green_empty[partner_ref[k], rows, window]
            out_ref[rows, window] = total * scale

    scale_rows(me)
    for c in range(CHUNKS):
        piece = pl.ds(c * size, size)
        pre_copy(c).wait_recv()
        cols[me, own_row, piece] = (mine[piece].astype(jnp.float32) + pre_in[piece].astype(jnp.float32)).astype(jnp.bfloat16)
        pl.when(me < last)(up_copy(0, c).start)
        pl.when(me > 0)(down_copy(0, c).start)
        cross_copy(me, c).start()
        if 0 < c < kpoints:
            for copy in row_copies(c):
                copy.wait_recv()
            for copy in row_forwards(c):
                copy.start()
    for d in range(CHUNKS, kpoints):
        for copy in row_copies(d):
            copy.wait_recv()
        for copy in row_forwards(d):
            copy.start()
    multiply(me, own_row)

    def partner_at(i):
        value, bit = me, 1
        while bit < kpoints:
            if i & bit:
                value = value + bit - 2 * bit * lax.rem(me // bit, 2)
            bit *= 2
        return value

    for s in range(last):
        for c in range(CHUNKS):
            @pl.when(me > s)
            def _():
                up_copy(s, c).wait_recv()
                pl.when(me < last)(up_copy(s + 1, c).start)
                cross_copy(lax.rem(me - 1 - s + kpoints, kpoints), c).start()

            @pl.when(me < last - s)
            def _():
                down_copy(s, c).wait_recv()
                pl.when(me > 0)(down_copy(s + 1, c).start)
                cross_copy(lax.rem(me + 1 + s, kpoints), c).start()
        if s == 0:
            for d in range(1, kpoints):
                for copy in row_forwards(d):
                    copy.wait_recv()
        source = partner_at(s + 1)
        scale_rows(source)
        multiply(source, own_row)
    combine(own_row)
    for i in range(kpoints):
        source = partner_at(i)
        for c in range(CHUNKS):
            cross_copy(source, c).wait_recv()
        multiply(source, 1 - own_row)
    combine(1 - own_row)

    for d in range(1, kpoints):
        for copy in row_copies(d) + row_forwards(d):
            copy.wait_send()
    for c in range(CHUNKS):
        pre_copy(c).wait_send()
        for k in range(kpoints):
            cross_copy(k, c).wait_send()
        for s in range(last):
            pl.when((me < last) & (me >= s))(up_copy(s, c).wait_send)
            pl.when((me > 0) & (me + s <= last))(down_copy(s, c).wait_send)


def line(occ, empty, occ_energy, empty_energy, tau_points, partner, mirror, kpoints, columns, scale):
    nrows, nocc = occ.shape
    nemp = empty.shape[1]
    width = nocc + nemp
    window, times = mirror.shape[0], tau_points.shape[0]
    half, slab = window // 2, nrows // kpoints
    part = slab // columns
    dma = pltpu.SemaphoreType.DMA
    vmem = pl.BlockSpec(memory_space=pltpu.VMEM)
    smem = pl.BlockSpec(memory_space=pltpu.SMEM)
    bf16, f32 = jnp.bfloat16, jnp.float32
    return pl.pallas_call(
        functools.partial(line_kernel, kpoints, columns, scale),
        out_shape=jax.ShapeDtypeStruct((times * slab, window), f32),
        in_specs=[smem, smem, vmem, vmem, vmem, vmem, vmem],
        out_specs=vmem,
        scratch_shapes=[
            pltpu.VMEM((kpoints, 2, half, width), bf16),
            pltpu.VMEM((half, width), bf16),
            pltpu.VMEM((half, width), bf16),
            pltpu.VMEM((half, width), bf16),
            pltpu.VMEM((kpoints, columns, part, nocc), bf16),
            pltpu.VMEM((kpoints, columns, part, nemp), bf16),
            pltpu.VMEM((kpoints, times * slab, nocc), bf16),
            pltpu.VMEM((kpoints, times * slab, nemp), bf16),
            pltpu.VMEM((kpoints, times * slab, window), f32),
            pltpu.VMEM((kpoints, times * slab, window), f32),
            dma((CHUNKS,)), dma((CHUNKS,)),
            dma((2, kpoints)), dma((2, kpoints)),
            dma((2, kpoints, columns)), dma((2, kpoints, columns)),
            dma((kpoints, CHUNKS)), dma((kpoints, CHUNKS)),
            dma((kpoints, CHUNKS)), dma((kpoints, CHUNKS)),
            dma((kpoints, CHUNKS)), dma((kpoints, CHUNKS)),
        ],
        compiler_params=pltpu.CompilerParams(collective_id=0, has_side_effects=True),
        name="line",
    )(tau_points, partner, mirror.reshape(1, window), occ_energy, empty_energy, occ, empty)


def shards_line(occ_orbitals, empty_orbitals, occ_energy, empty_energy, tau_points, partner, mirror):
    kpoints, columns = lax.axis_size("kpt"), lax.axis_size("col")
    scale = -1.0 / math.sqrt(kpoints) / math.sqrt(NOCC) / math.sqrt(NEMP)
    total = line(
        occ_orbitals[0], empty_orbitals[0], occ_energy, empty_energy, tau_points, partner, mirror,
        kpoints, columns, scale)
    return total.reshape(tau_points.shape[0], 1, -1, mirror.shape[0])


def shards(*args):
    kpoints, columns = lax.axis_size("kpt"), lax.axis_size("col")
    nrows, nocc, nemp = args[0].shape[1], args[0].shape[2], args[1].shape[2]
    times, window = args[4].shape[0], args[6].shape[0]
    slab, width = nrows // kpoints, nocc + nemp
    held = 2 * width * (kpoints * window + 4 * nrows + times * nrows) + 8 * times * nrows * window
    aligned = window % (2 * LANES) == 0 and nrows % LANES == 0 and nocc % LANES == 0 and nemp % LANES == 0
    aligned = aligned and (slab // columns) % 16 == 0 and slab % columns == 0 and nrows % kpoints == 0
    fits = aligned and held <= LINE_BYTES and kpoints & (kpoints - 1) == 0
    if lax.axis_size("row") == 2 and fits:
        return shards_line(*args)
    return shards_reduced(*args)


def solution(mesh):
    return jax.shard_map(
        shards,
        mesh=mesh,
        in_specs=(P("kpt", "row", None), P("kpt", "row", None), P(), P(), P(), P(), P("col")),
        out_specs=P(None, "row", "kpt", "col"),
        check_vma=False,
    )
```

time: 150 us -> 80.2 us (0.53)
  the two profiles are of different devices: /device:TPU:8 before, /device:TPU:0 now
where the time goes in v1:
time: 80.2 us; the launch traced here: 80 us
  Pallas kernels  77.3 us (96%)
  local copies, waits for them, and re-layouts  2.67 us (3%)
    pallas_call x1, Pallas kernels, line(): pl.pallas_call(functools.partial(line_kernel, kpoints, columns, scale), o...  77.3 us
    unnamed x1, local copies, waits for them, and re-layouts  2.67 us

profile of v1, /device:TPU:0, one launch (start us, length us, event | category | flops | bytes accessed | tf_op | source)
XLA Modules:
  0.0 80.0 jit_solution(15322116899191124503)
XLA Ops:
  0.0 77.3 %line.1 = f32[768,512]{1,0:T(8,128)} custom-call(f32[3]{0:T(128)} %tau_ref.1, s32[4]{0:T(128)} %partner_ref.1, s32[1,512]{1,0:T(1,128)} %bitcast.9, f32[4,256]{1,0:T(4,128)} %occ_energy_ref.1, f32[4,896]{1,0:T(4,128)} %empty_energy_ref.1, bf16[1024,256]{1,0:T(8,128)(2,1)} %bitcast.8, bf16[1024,896]{1,0:T(8,128)(2,1)} %bitcast.7), custom_call_target="tpu_custom_call" | custom-call | tf_op jit(solution)/shard_map/line/pallas_call | solution.py:274
  77.3 2.7 %copy.10 = f32[3,1,256,512]{3,2,1,0:T(8,128)} copy(f32[3,1,256,512]{3,2,1,0:T(8,128)} %bitcast.6) | data formatting | bytes 3145728

commit v2 on v1

--- a/solution.py
+++ b/solution.py
@@ -12,7 +12,9 @@
 NEMP = 896
 TAUS = 3
 LINE_BYTES = 40 * 2**20
+KERNEL_BYTES = 60 * 1024 * 2**10
 CHUNKS = 4
+EXTRAS = (1, 1, 0)
 LANES = 128
 TILE = 16
 
@@ -62,10 +64,11 @@
 
 
 def line_kernel(kpoints, columns, scale,
-                tau_ref, partner_ref, mirror_ref, occ_energy_ref, empty_energy_ref, occ_ref, empty_ref, out_ref,
+                tau_in, partner_in, mirror_in, occ_energy_in, empty_energy_in, occ_in, empty_in, out_ref,
+                tau_ref, partner_ref, mirror_ref, occ_energy_ref, empty_energy_ref, occ_ref, empty_ref, local_sem,
                 cols, mine, pre_out, pre_in, rows_occ, rows_empty, scaled_occ, scaled_empty, green_occ, green_empty,
                 send_p, recv_p, send_r, recv_r, send_f, recv_f,
-                send_u, recv_u, send_d, recv_d, send_x, recv_x):
+                send_u, recv_u, send_d, recv_d, send_x, recv_x, send_y, recv_y, send_z, recv_z):
     me, own_row, own_col = lax.axis_index("kpt"), lax.axis_index("row"), lax.axis_index("col")
     nrows, nocc = occ_ref.shape
     width = nocc + empty_ref.shape[1]
@@ -84,12 +87,22 @@
             device_id=device, device_id_type=pl.DeviceIdType.MESH,
         )
 
+    loads = [
+        pltpu.make_async_copy(src, dst, local_sem.at[i])
+        for i, (src, dst) in enumerate((
+            (mirror_in, mirror_ref), (occ_in, occ_ref), (empty_in, empty_ref), (occ_energy_in, occ_energy_ref),
+            (empty_energy_in, empty_energy_ref), (tau_in, tau_ref), (partner_in, partner_ref)))
+    ]
+    for copy in loads:
+        copy.start()
     barrier = pltpu.get_barrier_semaphore()
     peers = [{"kpt": lax.rem(me + d, kpoints)} for d in range(1, kpoints)]
     peers += [across]
     peers += [{"col": lax.rem(own_col + e, columns)} for e in range(1, columns)]
     for peer in peers:
         pl.semaphore_signal(barrier, inc=1, device_id=peer, device_id_type=pl.DeviceIdType.MESH)
+    for copy in loads:
+        copy.wait()
     pl.semaphore_wait(barrier, len(peers))
 
     def row_copies(d):
@@ -124,6 +137,31 @@
     def down_copy(s, c):
         piece = cols.at[lax.rem(me + s, kpoints), own_row, pl.ds(c * size, size)]
         return remote(piece, piece, send_d.at[s, c], recv_d.at[s, c], below)
+
+    def extras(s):
+        return EXTRAS[min(s, len(EXTRAS) - 1)] if s < last else 0
+
+    def extra_up(s, c):
+        piece = cols.at[lax.rem(me - s + kpoints, kpoints), 1 - own_row, pl.ds(c * size, size)]
+        return remote(piece, piece, send_y.at[s, c], recv_y.at[s, c], above)
+
+    def extra_down(s, c):
+        piece = cols.at[lax.rem(me + s, kpoints), 1 - own_row, pl.ds(c * size, size)]
+        return remote(piece, piece, send_z.at[s, c], recv_z.at[s, c], below)
+
+    def pass_extras(s):
+        for c in range(extras(s)):
+            @pl.when(me > s)
+            def _():
+                extra_up(s, c).wait_recv()
+                if c < extras(s + 1):
+                    pl.when(me < last)(extra_up(s + 1, c).start)
+
+            @pl.when(me < last - s)
+            def _():
+                extra_down(s, c).wait_recv()
+                if c < extras(s + 1):
+                    pl.when(me > 0)(extra_down(s + 1, c).start)
 
     for d in range(1, kpoints):
         for copy in row_copies(d):
@@ -226,13 +264,15 @@
             def _():
                 up_copy(s, c).wait_recv()
                 pl.when(me < last)(up_copy(s + 1, c).start)
-                cross_copy(lax.rem(me - 1 - s + kpoints, kpoints), c).start()
+                if c >= extras(s):
+                    cross_copy(lax.rem(me - 1 - s + kpoints, kpoints), c).start()
 
             @pl.when(me < last - s)
             def _():
                 down_copy(s, c).wait_recv()
                 pl.when(me > 0)(down_copy(s + 1, c).start)
-                cross_copy(lax.rem(me + 1 + s, kpoints), c).start()
+                if c >= extras(s):
+                    cross_copy(lax.rem(me + 1 + s, kpoints), c).start()
         if s == 0:
             for d in range(1, kpoints):
                 for copy in row_forwards(d):
@@ -240,12 +280,27 @@
         source = partner_at(s + 1)
         scale_rows(source)
         multiply(source, own_row)
+        if s == 0:
+            for c in range(CHUNKS):
+                cross_copy(me, c).wait_recv()
+                if c < extras(0):
+                    pl.when(me < last)(extra_up(0, c).start)
+                    pl.when(me > 0)(extra_down(0, c).start)
+            multiply(me, 1 - own_row)
+        else:
+            pass_extras(s - 1)
     combine(own_row)
-    for i in range(kpoints):
-        source = partner_at(i)
-        for c in range(CHUNKS):
-            cross_copy(source, c).wait_recv()
-        multiply(source, 1 - own_row)
+    pass_extras(last - 1)
+    for s in range(last):
+        for c in range(extras(s), CHUNKS):
+            @pl.when(me > s)
+            def _():
+                cross_copy(lax.rem(me - 1 - s + kpoints, kpoints), c).wait_recv()
+
+            @pl.when(me < last - s)
+            def _():
+                cross_copy(lax.rem(me + 1 + s, kpoints), c).wait_recv()
+        multiply(partner_at(s + 1), 1 - own_row)
     combine(1 - own_row)
 
     for d in range(1, kpoints):
@@ -253,9 +308,14 @@
             copy.wait_send()
     for c in range(CHUNKS):
         pre_copy(c).wait_send()
-        for k in range(kpoints):
-            cross_copy(k, c).wait_send()
+        cross_copy(me, c).wait_send()
         for s in range(last):
+            if c >= extras(s):
+                pl.when(me > s)(cross_copy(lax.rem(me - 1 - s + kpoints, kpoints), c).wait_send)
+                pl.when(me < last - s)(cross_copy(lax.rem(me + 1 + s, kpoints), c).wait_send)
+            else:
+                pl.when((me < last) & (me >= s))(extra_up(s, c).wait_send)
+                pl.when((me > 0) & (me + s <= last))(extra_down(s, c).wait_send)
             pl.when((me < last) & (me >= s))(up_copy(s, c).wait_send)
             pl.when((me > 0) & (me + s <= last))(down_copy(s, c).wait_send)
 
@@ -268,15 +328,22 @@
     half, slab = window // 2, nrows // kpoints
     part = slab // columns
     dma = pltpu.SemaphoreType.DMA
-    vmem = pl.BlockSpec(memory_space=pltpu.VMEM)
-    smem = pl.BlockSpec(memory_space=pltpu.SMEM)
+    hbm = pl.BlockSpec(memory_space=pltpu.HBM)
     bf16, f32 = jnp.bfloat16, jnp.float32
     return pl.pallas_call(
         functools.partial(line_kernel, kpoints, columns, scale),
         out_shape=jax.ShapeDtypeStruct((times * slab, window), f32),
-        in_specs=[smem, smem, vmem, vmem, vmem, vmem, vmem],
-        out_specs=vmem,
+        in_specs=[hbm] * 7,
+        out_specs=pl.BlockSpec(memory_space=pltpu.VMEM),
         scratch_shapes=[
+            pltpu.SMEM((times,), f32),
+            pltpu.SMEM((kpoints,), jnp.int32),
+            pltpu.VMEM((1, window), jnp.int32),
+            pltpu.VMEM(occ_energy.shape, f32),
+            pltpu.VMEM(empty_energy.shape, f32),
+            pltpu.VMEM(occ.shape, bf16),
+            pltpu.VMEM(empty.shape, bf16),
+            dma((7,)),
             pltpu.VMEM((kpoints, 2, half, width), bf16),
             pltpu.VMEM((half, width), bf16),
             pltpu.VMEM((half, width), bf16),
@@ -293,8 +360,10 @@
             dma((kpoints, CHUNKS)), dma((kpoints, CHUNKS)),
             dma((kpoints, CHUNKS)), dma((kpoints, CHUNKS)),
             dma((kpoints, CHUNKS)), dma((kpoints, CHUNKS)),
+            dma((kpoints, CHUNKS)), dma((kpoints, CHUNKS)),
+            dma((kpoints, CHUNKS)), dma((kpoints, CHUNKS)),
         ],
-        compiler_params=pltpu.CompilerParams(collective_id=0, has_side_effects=True),
+        compiler_params=pltpu.CompilerParams(collective_id=0, has_side_effects=True, vmem_limit_bytes=KERNEL_BYTES),
         name="line",
     )(tau_points, partner, mirror.reshape(1, window), occ_energy, empty_energy, occ, empty)
 

time: 80.2 us -> 72.7 us (0.906)
  Pallas kernels: 77.3 us -> 69.9 us
    pallas_call x1, Pallas kernels: 77.3 us -> 69.9 us  [line(): pl.pallas_call(functools.partial(line_kernel, kpoints, columns, scale), o...]
where the time goes in v2:
time: 72.7 us; the launch traced here: 72.6 us
  Pallas kernels  69.9 us (96%)
  local copies, waits for them, and re-layouts  2.67 us (4%)
    pallas_call x1, Pallas kernels, line(): pl.pallas_call(functools.partial(line_kernel, kpoints, columns, scale), o...  69.9 us
    unnamed x1, local copies, waits for them, and re-layouts  2.67 us

profile of v2, /device:TPU:0, one launch (start us, length us, event | category | flops | bytes accessed | tf_op | source)
XLA Modules:
  0.0 72.6 jit_solution(16284866991100674919)
XLA Ops:
  0.0 69.9 %line.1 = f32[768,512]{1,0:T(8,128)} custom-call(f32[3]{0:T(128)} %tau_in.1, s32[4]{0:T(128)} %partner_in.1, s32[1,512]{1,0:T(1,128)} %bitcast.9, f32[4,256]{1,0:T(4,128)} %occ_energy_in.1, f32[4,896]{1,0:T(4,128)} %empty_energy_in.1, bf16[1024,256]{1,0:T(8,128)(2,1)} %bitcast.8, bf16[1024,896]{1,0:T(8,128)(2,1)} %bitcast.7), custom_call_target="tpu_custom_call" | custom-call | tf_op jit(solution)/shard_map/line/pallas_call | solution.py:333
  69.9 2.7 %copy.10 = f32[3,1,256,512]{3,2,1,0:T(8,128)} copy(f32[3,1,256,512]{3,2,1,0:T(8,128)} %bitcast.6) | data formatting | bytes 3145728

commit v3 on v2

--- a/solution.py
+++ b/solution.py
@@ -12,7 +12,7 @@
 NEMP = 896
 TAUS = 3
 LINE_BYTES = 40 * 2**20
-KERNEL_BYTES = 60 * 1024 * 2**10
+KERNEL_BYTES = 48 * 2**20
 CHUNKS = 4
 EXTRAS = (1, 1, 0)
 LANES = 128
@@ -103,7 +103,6 @@
         pl.semaphore_signal(barrier, inc=1, device_id=peer, device_id_type=pl.DeviceIdType.MESH)
     for copy in loads:
         copy.wait()
-    pl.semaphore_wait(barrier, len(peers))
 
     def row_copies(d):
         other = lax.rem(me + d, kpoints)
@@ -163,9 +162,6 @@
                 if c < extras(s + 1):
                     pl.when(me > 0)(extra_down(s + 1, c).start)
 
-    for d in range(1, kpoints):
-        for copy in row_copies(d):
-            copy.start()
 
     def pick(first):
         index = mirror_ref[0:1, pl.ds(pl.multiple_of(first, LANES), LANES)] - own_row * nrows
@@ -183,7 +179,15 @@
             dst[first:first + LANES, nocc:] = empty
             yield range(first // size, (first + LANES) // size)
 
-    for chunks in fill(pre_out, 1 - own_row):
+    filling = fill(pre_out, 1 - own_row)
+    ready = next(filling)
+    pl.semaphore_wait(barrier, len(peers))
+    for c in ready:
+        pre_copy(c).start()
+    for d in range(1, kpoints):
+        for copy in row_copies(d):
+            copy.start()
+    for chunks in filling:
         for c in chunks:
             pre_copy(c).start()
     for _ in fill(mine, own_row):
@@ -365,7 +369,10 @@
         ],
         compiler_params=pltpu.CompilerParams(collective_id=0, has_side_effects=True, vmem_limit_bytes=KERNEL_BYTES),
         name="line",
-    )(tau_points, partner, mirror.reshape(1, window), occ_energy, empty_energy, occ, empty)
+    )(*(
+        pltpu.with_memory_space_constraint(operand, pltpu.HBM)
+        for operand in (tau_points, partner, mirror.reshape(1, window), occ_energy, empty_energy, occ, empty)
+    ))
 
 
 def shards_line(occ_orbitals, empty_orbitals, occ_energy, empty_energy, tau_points, partner, mirror):

time: 72.7 us -> 69.5 us (0.956)
  Pallas kernels: 69.9 us -> 68.2 us
  local copies, waits for them, and re-layouts: 2.67 us -> 1.15 us
    pallas_call x1, Pallas kernels: 69.9 us -> 68.2 us  [line(): pl.pallas_call(functools.partial(line_kernel, kpoints, columns, scale), o...]
    unnamed x1, local copies, waits for them, and re-layouts: 2.67 us -> 1.15 us
where the time goes in v3:
time: 69.5 us; the launch traced here: 69.3 us
  Pallas kernels  68.2 us (98%)
  local copies, waits for them, and re-layouts  1.15 us (2%)
    pallas_call x1, Pallas kernels, line(): pl.pallas_call(functools.partial(line_kernel, kpoints, columns, scale), o...  68.2 us

profile of v3, /device:TPU:0, one launch (start us, length us, event | category | flops | bytes accessed | tf_op | source)
XLA Modules:
  0.0 69.3 jit_solution(12513143824387889175)
XLA Ops:
  0.0 68.2 %line.1 = f32[768,512]{1,0:T(8,128)S(1)} custom-call(f32[3]{0:T(128)} %tau_in.1, s32[4]{0:T(128)} %partner_in.1, s32[1,512]{1,0:T(1,128)} %bitcast.9, f32[4,256]{1,0:T(4,128)} %occ_energy_in.1, f32[4,896]{1,0:T(4,128)} %empty_energy_in.1, bf16[1024,256]{1,0:T(8,128)(2,1)} %bitcast.8, bf16[1024,896]{1,0:T(8,128)(2,1)} %bitcast.7), custom_call_target="tpu_custom_call" | custom-call | tf_op jit(solution)/shard_map/line/pallas_call | solution.py:337
  68.2 1.1 %copy.10 = f32[3,1,256,512]{3,2,1,0:T(8,128)} copy(f32[3,1,256,512]{3,2,1,0:T(8,128)S(1)} %bitcast.6) | data formatting | bytes 3145728

commit v4 on v3

--- a/solution.py
+++ b/solution.py
@@ -129,6 +129,10 @@
         piece = cols.at[k, own_row, pl.ds(c * size, size)]
         return remote(piece, piece, send_x.at[k, c], recv_x.at[k, c], across)
 
+    def own_cross(g):
+        piece = cols.at[me, own_row, pl.ds(g * 2 * size, 2 * size)]
+        return remote(piece, piece, send_x.at[me, g], recv_x.at[me, g], across)
+
     def up_copy(s, c):
         piece = cols.at[lax.rem(me - s + kpoints, kpoints), own_row, pl.ds(c * size, size)]
         return remote(piece, piece, send_u.at[s, c], recv_u.at[s, c], above)
@@ -212,19 +216,19 @@
                     start = pl.multiple_of(t * slab + c * part, part)
                     scaled[k, pl.ds(start, part), :] = (block * weights[t]).astype(jnp.bfloat16)
 
-    def multiply(k, h):
-        window = pl.ds(pl.multiple_of(h * half, half), half)
+    def multiply(k, h, lo_slot=0, slots=half):
+        window = pl.ds(pl.multiple_of(h * half + lo_slot, slots), slots)
 
         @pl.loop(0, times)
         def _(t):
             rows = pl.ds(pl.multiple_of(t * slab, slab), slab)
             for scaled, green, lo, hi in ((scaled_occ, green_occ, 0, nocc), (scaled_empty, green_empty, nocc, width)):
                 green[k, rows, window] = lax.dot_general(
-                    scaled[k, rows, :], cols[k, h, :, lo:hi], (((1,), (1,)), ((), ())),
+                    scaled[k, rows, :], cols[k, h, lo_slot:lo_slot + slots, lo:hi], (((1,), (1,)), ((), ())),
                     preferred_element_type=jnp.float32)
 
-    def combine(h):
-        window = pl.ds(pl.multiple_of(h * half, half), half)
+    def combine(h, lo_slot=0, slots=half):
+        window = pl.ds(pl.multiple_of(h * half + lo_slot, slots), slots)
 
         @pl.loop(0, times * slab, step=TILE)
         def _(start):
@@ -241,7 +245,8 @@
         cols[me, own_row, piece] = (mine[piece].astype(jnp.float32) + pre_in[piece].astype(jnp.float32)).astype(jnp.bfloat16)
         pl.when(me < last)(up_copy(0, c).start)
         pl.when(me > 0)(down_copy(0, c).start)
-        cross_copy(me, c).start()
+        if c % 2:
+            own_cross(c // 2).start()
         if 0 < c < kpoints:
             for copy in row_copies(c):
                 copy.wait_recv()
@@ -281,22 +286,28 @@
             for d in range(1, kpoints):
                 for copy in row_forwards(d):
                     copy.wait_recv()
+        if s == min(1, last - 1):
+            if s == 0:
+                for g in range(CHUNKS // 2):
+                    own_cross(g).wait_recv()
+            for c in range(extras(0)):
+                pl.when(me < last)(extra_up(0, c).start)
+                pl.when(me > 0)(extra_down(0, c).start)
         source = partner_at(s + 1)
         scale_rows(source)
         multiply(source, own_row)
         if s == 0:
-            for c in range(CHUNKS):
-                cross_copy(me, c).wait_recv()
-                if c < extras(0):
-                    pl.when(me < last)(extra_up(0, c).start)
-                    pl.when(me > 0)(extra_down(0, c).start)
+            if last > 1:
+                for g in range(CHUNKS // 2):
+                    own_cross(g).wait_recv()
             multiply(me, 1 - own_row)
-        else:
-            pass_extras(s - 1)
+        if s > 1:
+            pass_extras(s - 2)
     combine(own_row)
-    pass_extras(last - 1)
-    for s in range(last):
-        for c in range(extras(s), CHUNKS):
+    for s in range(max(last - 2, 0), last):
+        pass_extras(s)
+    def take_crossed(s, chunks):
+        for c in chunks:
             @pl.when(me > s)
             def _():
                 cross_copy(lax.rem(me - 1 - s + kpoints, kpoints), c).wait_recv()
@@ -304,15 +315,22 @@
             @pl.when(me < last - s)
             def _():
                 cross_copy(lax.rem(me + 1 + s, kpoints), c).wait_recv()
+
+    for s in range(last - 1):
+        take_crossed(s, range(extras(s), CHUNKS))
         multiply(partner_at(s + 1), 1 - own_row)
-    combine(1 - own_row)
+    for first in range(0, half, LANES):
+        take_crossed(last - 1, range(max(extras(last - 1), first // size), (first + LANES) // size))
+        multiply(partner_at(last), 1 - own_row, first, LANES)
+        combine(1 - own_row, first, LANES)
 
     for d in range(1, kpoints):
         for copy in row_copies(d) + row_forwards(d):
             copy.wait_send()
     for c in range(CHUNKS):
         pre_copy(c).wait_send()
-        cross_copy(me, c).wait_send()
+        if c % 2:
+            own_cross(c // 2).wait_send()
         for s in range(last):
             if c >= extras(s):
                 pl.when(me > s)(cross_copy(lax.rem(me - 1 - s + kpoints, kpoints), c).wait_send)

time: 69.5 us -> 69.3 us (level)
  no operation moved by 1% of the time
where the time goes in v4:
time: 69.3 us; the launch traced here: 69.1 us
  Pallas kernels  68 us (98%)
  local copies, waits for them, and re-layouts  1.15 us (2%)
    pallas_call x1, Pallas kernels, line(): pl.pallas_call(functools.partial(line_kernel, kpoints, columns, scale), o...  68 us

profile of v4, /device:TPU:0, one launch (start us, length us, event | category | flops | bytes accessed | tf_op | source)
XLA Modules:
  0.0 69.1 jit_solution(5212792377423934391)
XLA Ops:
  0.0 68.0 %line.1 = f32[768,512]{1,0:T(8,128)S(1)} custom-call(f32[3]{0:T(128)} %tau_in.1, s32[4]{0:T(128)} %partner_in.1, s32[1,512]{1,0:T(1,128)} %bitcast.9, f32[4,256]{1,0:T(4,128)} %occ_energy_in.1, f32[4,896]{1,0:T(4,128)} %empty_energy_in.1, bf16[1024,256]{1,0:T(8,128)(2,1)} %bitcast.8, bf16[1024,896]{1,0:T(8,128)(2,1)} %bitcast.7), custom_call_target="tpu_custom_call" | custom-call | tf_op jit(solution)/shard_map/line/pallas_call | solution.py:355
  68.0 1.1 %copy.10 = f32[3,1,256,512]{3,2,1,0:T(8,128)} copy(f32[3,1,256,512]{3,2,1,0:T(8,128)S(1)} %bitcast.6) | data formatting | bytes 3145728
